TPU v7x, 32 devices: a 4x4x1 block of a 4x4x8 slice. The times are simulated.
32 devices in a mesh: dp: 2 (over z, core), tp: 16 (over x, y).
Axes of the slice: x: 4, y: 4, z: 1, core: 2. Of those that a mesh axis runs over, the one named last changes fastest.
The devices are a block of a 4x4x8 slice.
Arguments:
- x: bfloat16 [5120, 7168], P(('dp', 'tp')), parts along dimension 0
- w_gate: bfloat16 [7168, 18432], P(None, 'tp')
- w_up: bfloat16 [7168, 18432], P(None, 'tp')
- w_down: bfloat16 [18432, 7168], P('tp')
Outputs:
- output: bfloat16 [5120, 7168], P(('dp', 'tp')), parts along dimension 0
There are 2 independent parts. A program takes and returns all parts, laid end to end along the dimension named above; an argument that names none is the same for every part.
All inputs are finite; a program needn't handle non-finite values.
Results may differ from a plain program's by a relative error of at most 0.016.
Values are sent between devices in bfloat16 or wider.
A program may use at most 768 MiB of HBM per device.

v0:
```python
import jax
import jax.numpy as jnp
from jax import lax
from jax.sharding import PartitionSpec as P


def solution(mesh):
    def step(x, w_gate, w_up, w_down):
        rows = lax.all_gather(x, "tp", axis=0, tiled=True)
        gate = jnp.dot(rows, w_gate, preferred_element_type=jnp.float32)
        up = jnp.dot(rows, w_up, preferred_element_type=jnp.float32)
        hidden = (jax.nn.silu(gate) * up).astype(jnp.bfloat16)
        term = jnp.dot(hidden, w_down, preferred_element_type=jnp.float32).astype(jnp.bfloat16)
        return lax.psum_scatter(term, "tp", scatter_dimension=0, tiled=True)

    return jax.shard_map(
        step,
        mesh=mesh,
        in_specs=(P(("dp", "tp"), None), P(None, "tp"), P(None, "tp"), P("tp", None)),
        out_specs=P(("dp", "tp"), None),
        check_vma=False,
    )
```

profile of v0, /device:TPU:96, one launch (start us, length us, event | category | flops | bytes accessed | tf_op | source)
XLA Modules:
  0.0 600.8 jit_solution(5708407512712889847)
XLA Ops:
  6.5 0.0 all-gather.2.cloned.1.call-start
  6.6 0.7 all-gather.2.cloned.1.call-update
  7.3 0.1 reduce-scatter.2.cloned.1.call-start
  7.4 212.5 %all-gather.2.cloned.1.call-done = bf16[2560,7168]{1,0:T(8,128)(2,1)} async-done(((bf16[160,7168]{1,0:T(8,128)(2,1)}), bf16[2560,7168]{1,0:T(8,128)(2,1)}) %all-gather.2.cloned.1.call-update) | async-done | bytes 36700176 | tf_op jit(solution)/shard_map/all_gather | solution.py:9
  219.8 57.3 %fusion.1 = f32[2560,1152]{1,0:T(8,128)} fusion(bf16[2560,7168]{1,0:T(8,128)(2,1)} %all-gather.2.cloned.1.call-done, bf16[7168,1152]{1,0:T(8,128)(2,1)} %param.5), kind=kOutput, calls=%fused_computation.3 | convolution fusion | flops 42278584320 | bytes 65011712 | tf_op jit(solution)/shard_map/dot_general | solution.py:10
  277.1 56.8 %fusion = bf16[2560,1152]{1,0:T(8,128)(2,1)S(1)} fusion(bf16[2560,7168]{1,0:T(8,128)(2,1)} %all-gather.2.cloned.1.call-done, bf16[7168,1152]{1,0:T(8,128)(2,1)} %param.6, f32[2560,1152]{1,0:T(8,128)} %fusion.1), kind=kOutput, calls=%fused_computation.2 | convolution fusion | flops 42296279040 | bytes 70909952 | tf_op jit(solution)/shard_map/dot_general | solution.py:11
  333.9 54.6 %convolution_convert_fusion = bf16[2560,7168]{1,0:T(8,128)(2,1)} fusion(bf16[2560,1152]{1,0:T(8,128)(2,1)S(1)} %fusion, bf16[1152,7168]{1,0:T(8,128)(2,1)} %param.7), kind=kOutput, calls=%fused_computation | convolution fusion | flops 42296934400 | bytes 59113472 | tf_op jit(solution)/shard_map/dot_general | solution.py:13
  388.5 0.1 reduce-scatter.2.cloned.1.call-update
  388.6 205.3 %reduce-scatter.2.cloned.1.call-done = bf16[160,7168]{1,0:T(8,128)(2,1)} async-done(((bf16[2560,7168]{1,0:T(8,128)(2,1)}), bf16[160,7168]{1,0:T(8,128)(2,1)}) %reduce-scatter.2.cloned.1.call-update) | async-done | bytes 2293776 | tf_op jit(solution)/shard_map/reduce_scatter | solution.py:14
Async XLA Ops:
  6.5 213.3 %all-gather.2.cloned.1.call-start = ((), (), s32[]{:S(2)}) async-start(), calls=%async_computation.1 | async-start | bytes 38993920 | tf_op jit(solution)/shard_map/all_gather | solution.py:9
  7.3 586.6 %reduce-scatter.2.cloned.1.call-start = ((), (), s32[]{:S(2)}) async-start(), calls=%async_computation.2 | async-start | bytes 38993920 | tf_op jit(solution)/shard_map/reduce_scatter | solution.py:14
Sparse Core Ops, SparseCore 0:
  9.3 210.4 all-gather.1
  388.7 205.1 reduce-scatter.1
where the time goes:
time: 602 us; the launch traced here: 601 us
  waiting for transfers between devices  419 us (70%)
  matrix products  169 us (28%)
  between operations  13.4 us (2%)
    all_gather x1, waiting for transfers between devices, step(): rows = lax.all_gather(x, 'tp', axis=0, tiled=True)  212 us
    reduce_scatter x1, waiting for transfers between devices, step(): return lax.psum_scatter(term, 'tp', scatter_dimension=0, tiled=True)  205 us
    dot_general x1, matrix products, step(): gate = jnp.dot(rows, w_gate, preferred_element_type=jnp.float32)  57.3 us
    dot_general x1, matrix products, step(): up = jnp.dot(rows, w_up, preferred_element_type=jnp.float32)  56.8 us
    dot_general x1, matrix products, step(): jnp.dot(hidden, w_down, preferred_element_type=jnp.float32)  54.6 us
  transfers between devices with their start and end apart: 2, of which 2 were waited for; matrix products, arithmetic and copies ran while one was open for 0% of the time, Pallas kernels for 0%

commit v1 on v0

v1 whole, which is shorter than its diff:
```python
import functools
import math

import jax
import jax.numpy as jnp
from jax import lax
from jax.experimental import pallas as pl
from jax.experimental.pallas import tpu as pltpu
from jax.sharding import PartitionSpec as P

MESH = pl.DeviceIdType.MESH
LANES = 128
EPOCHS = 2
OWN, OTHER = 0, 1
SLOTS = 8
TASK_SLOTS = ((0, 1, 2, 6), (3, 7, 4, 5))
GROUP_TILES = 3
LAG = 2
NB = 8
CHUNKS = 4
VLIM = 64600000


FIRST_U, BY_PARTNER = (14, 17), 2
TUNE = {'due_w': (95, 74), 'due_f': (70, 240), 'due_p': 815, 'due_h': (790, -30, 410, -30, 570, -170, 190, -130), 'backlog': 32.0, 'prefer': 438, 'phase': (1, 3, 3, 0.5)}


def columns(depth):
    t, (own, other) = depth // 28, FIRST_U
    end = 28 - BY_PARTNER
    return {
        OWN: ((0, own * t), (own * t, (28 - own) * t), None),
        OTHER: ((0, other * t), (other * t, (end - other) * t), (end * t, BY_PARTNER * t)),
    }


def gather_messages(depth, rows):
    msgs, deps = {}, {}
    re = rows // EPOCHS
    cols = columns(depth)

    def add(name, link, cls, src, dst, r, c, dep):
        msgs[name] = (link, cls, src, dst, r, c)
        deps[name] = dep

    for e in range(EPOCHS):
        every, a, b = (e * re, re), (e * re, re // 2), (e * re + re // 2, re // 2)
        add(("P1", OTHER, e), "P", OWN, 0, 0, every, cols[OTHER][0], [])
        add(("P2", OTHER, e), "P", OWN, 0, 0, every, (cols[OTHER][1][0], depth - cols[OTHER][1][0]), [])
        for cls in (OWN, OTHER):
            u, y, _ = cols[cls]
            m = lambda name: (name, cls, e)
            own_u = [] if cls == OWN else [("P1", OTHER, e)]
            own_y = [] if cls == OWN else [("P2", OTHER, e)]
            add(m("U1"), "U", cls, 0, 1, every, u, own_u)
            add(m("N1"), "N", cls, 0, 6, every, u, own_u)
            add(m("S1"), "S", cls, 0, 2, every, u, own_u)
            add(m("U2"), "U", cls, 0, 1, every, y, own_y)
            add(m("N2"), "N", cls, 0, 6, every, y, own_y)
            add(m("S2"), "S", cls, 0, 2, every, y, own_y)
            add(m("N3"), "N", cls, 1, 7, every, u, [m("U1")])
            add(m("S3"), "S", cls, 1, 3, every, u, [m("U1")])
            add(m("N4"), "N", cls, 6, 4, a, u, [m("N1")])
            add(m("S4"), "S", cls, 2, 4, b, u, [m("S1")])
            add(m("N5"), "N", cls, 6, 4, a, y, [m("N2")])
            add(m("S5"), "S", cls, 2, 4, b, y, [m("S2")])
            add(m("U3"), "U", cls, 6, 7, every, y, [m("N2")])
            add(m("U4"), "U", cls, 2, 3, every, y, [m("S2")])
            add(m("N6"), "N", cls, 7, 5, a, u, [m("N3")])
            add(m("S6"), "S", cls, 3, 5, b, u, [m("S3")])
            add(m("U5"), "U", cls, 4, 5, a, y, [m("N5")])
            add(m("U6"), "U", cls, 4, 5, b, y, [m("S5")])
        last = {1: ["U2"], 6: ["N2"], 2: ["S2"], 7: ["U3"], 3: ["U4"], 4: ["N5", "S5"], 5: ["U5", "U6"]}
        for s, need in last.items():
            add((f"F{s}", OTHER, e), "P", OWN, s, s, every, cols[OTHER][2], [(n, OWN, e) for n in need])
    return msgs, deps


def kind_of(message):
    to, cls, _, _, (_, r), cols = message
    return "P" if to == "P" else cls, r, cols


def send_kinds(msgs):
    return sorted({kind_of(m) for m in msgs.values()}, key=str)


def plan(depth, rows, width):
    rate, delay, tile_us, gt = 46.6e3, 2.2, 1.46, GROUP_TILES
    due_w, due_f, due_p, due_h, backlog = (TUNE[k] for k in ("due_w", "due_f", "due_p", "due_h", "backlog"))
    msgs, deps = gather_messages(depth, rows)
    pending = {name: set(d) for name, d in deps.items()}
    lack = {}
    for name, (link, cls, src, dst, r, c) in msgs.items():
        where = (OTHER if link == "P" else cls, name[2], dst)
        lack.setdefault(where, set()).add(name)
    pieces = depth // 4 // 256
    tasks = [(cls, e, h) for e in range(EPOCHS) for cls in (OWN, OTHER) for h in range(2)]
    subs = width // LANES // gt
    re, unit = rows // EPOCHS, depth // 28
    ncu, ncy = 8 * unit // CHUNKS, 6 * unit // CHUNKS
    nsteps = 2 * EPOCHS * CHUNKS
    copies = {}
    for i, (name, (link, cls, _, dst, (_, r), (_, c))) in enumerate(msgs.items()):
        e = name[2]
        if name[0][0] == "P":
            rank = due_p * e
        elif name[0][0] == "F":
            rank = due_f[e] + (15 if dst in TASK_SLOTS[1] else 0)
        else:
            rank = TUNE["phase"][2 * e + cls] * 1000 + i
        copies[name] = (link, r * c * 2, rank)
    for k in range(pieces):
        copies["W", k] = ("P", width * 256 * 2, due_w[0] + due_w[1] * k)
    for t in range(len(tasks)):
        copies["H", t] = ("P", 4 * re * width * 2, due_h[t] + 10 * t)
    parts = {
        0: ("N", re * ncu), 1: ("S", re * ncu), 2: ("U", 4 * re * ncy),
        3: ("N", 2 * re * ncu), 4: ("S", 2 * re * ncu), 5: ("N", re // 2 * ncy), 6: ("S", re // 2 * ncy),
        7: ("U", re * ncu), 8: ("N", re * ncy), 9: ("S", re * ncy),
    }
    stages = (((0, 1, 2), 1.65, ()), ((3, 4, 5, 6), 1.75, (0, 1, 2)), ((7, 8, 9), 1.35, (3, 4, 5, 6)), ((), 1.0, (7, 8, 9)))
    free = dict.fromkeys("NSUPC", 0.0)
    avail = [n for n in msgs if not pending[n]] + [("W", k) for k in range(pieces)]
    now, arrivals = 0.0, []
    arrived = {}
    steps, ops = [], []
    loaded = {}
    task = sub = it = forwarded = 0

    def emit(*op):
        ops.append(op)

    def post(link, nbytes, what, at=None):
        free[link] = max(now if at is None else at, free[link]) + nbytes / (rate if link != "C" else 300e3)
        arrived[what] = free[link] + delay
        if what[0] not in "DHBE":
            arrivals.append((free[link] + delay, what))

    def issue():
        for n in sorted(avail, key=lambda n: copies[n][2]):
            link, nbytes, _ = copies[n]
            if free[link] - now < backlog:
                avail.remove(n)
                emit({"W": "wsend", "H": "hsend"}.get(n[0], "send"), n[1] if n[0] in "WH" else n)
                post(link, nbytes, n)
        for k in range(task, min(task + 2, len(tasks))):
            cls, e, h = tasks[k]
            for i, s in enumerate(TASK_SLOTS[h]):
                if (k, i) not in loaded and not lack.get((cls, e, s)):
                    loaded[k, i] = now + 1.5
                    emit("load", k, i)

    INF = 1e9

    def b_ready():
        t = 0.0
        if it < nsteps:
            g = it // CHUNKS
            if it % CHUNKS == 0:
                e, cls = g // 2, 1 - g % 2
                if task <= e * 4 + cls * 2 + 1 or forwarded < pieces:
                    return INF
                for k in range(2):
                    t = max(t, arrived.get(("H", 2 * g + k), INF))
            if it == 0:
                t = max(t, max(arrived["D", k] for k in range(pieces)))
        for j in (1, 2, 3):
            s = it - j * LAG
            if 0 <= s < nsteps:
                for k in stages[j][2]:
                    t = max(t, arrived["B", k, s])
        return t

    while task < len(tasks) or it < nsteps + 3 * LAG:
        issue()
        for a in sorted((a for a in arrivals if a[0] <= now), key=lambda a: a[0]):
            arrivals.remove(a)
            what = a[1]
            now += 0.03
            emit("recv", what)
            if what[0] == "W":
                emit("forward", what[1])
                forwarded += 1
                post("C", width * 256 * 2, ("D", what[1]))
            else:
                for s in lack.values():
                    s.discard(what)
                for n in msgs:
                    if what in pending[n]:
                        pending[n].discard(what)
                        if not pending[n]:
                            avail.append(n)
            issue()
        tile_at = INF
        if task < len(tasks) and all((task, i) in loaded for i in range(4)):
            tile_at = max(loaded[task, i] for i in range(4))
        b_at = b_ready() if it < nsteps + 3 * LAG else INF
        choice = None
        if b_at <= now and tile_at <= now:
            busy = min(free["N"], free["U"]) - now
            choice = "B" if busy < TUNE["prefer"] else "T"
        elif b_at <= now:
            choice = "B"
        elif tile_at <= now:
            choice = "T"
        if choice == "T":
            steps.append((ops, "T"))
            ops = []
            now += gt * tile_us
            sub += 1
            if sub == subs:
                avail.append(("H", task))
                task, sub = task + 1, 0
            continue
        if choice == "B":
            steps.append((ops, "B"))
            ops = []
            for j in (3, 2, 1, 0):
                s = it - j * LAG
                if 0 <= s < nsteps:
                    now += stages[j][1]
                    for k in stages[j][0]:
                        link, n = parts[k]
                        post(link, 2 * n, ("B", k, s))
                    if j == 3 and s // CHUNKS % 2 == 0:
                        post("P", 2 * re * (ncu + ncy), ("E", s))
            now += 0.1
            it += 1
            continue
        times = [a[0] for a in arrivals] + [t for t in (tile_at, b_at) if t < INF]
        if avail:
            times.append(min(max(now + 0.3, free[copies[n][0]] - backlog + 0.1) for n in avail))
        now = max(now, min(times))
    assert not avail and not arrivals, (avail, arrivals)
    steps.append((ops, ""))
    return steps


def kernel(n, steps_, msgs, x_hbm, gate_hbm, up_hbm, down_hbm, out, xl, gbuf, w, xbuf, hid,
           lu1, lu2, lu3, ly1, ly2, ly3, tu1, tu2, tu3, ty1, ty2, ty3, tq,
           gsend, grecv, xsem, gusem, wosem, wsend, wrecv, dsend, drecv, hsend, hrecv,
           bsend, brecv, fsend, frecv):
    rows, depth = x_hbm.shape
    width = gate_hbm.shape[1]
    re, half = rows // EPOCHS, depth // 2
    quarter, hr = half // 2, re // 2
    tiles = width // LANES
    pieces = quarter // 256
    unit = depth // 28
    ncu, ncy = 8 * unit // CHUNKS, 6 * unit // CHUNKS
    tasks = [(cls, e, h) for e in range(EPOCHS) for cls in (OWN, OTHER) for h in range(2)]
    total_tiles = len(tasks) * tiles
    steps = 2 * EPOCHS * CHUNKS

    side = math.isqrt(n)
    me, dp = lax.axis_index("tp"), lax.axis_index("dp")
    x, y = me // side, me % side
    role, core = ((x + 1) // 2) % 2, dp % 2
    link = {
        "N": {"tp": x * side + (y + 1) % side},
        "S": {"tp": x * side + (y + side - 1) % side},
        "U": {"tp": (side - 1 - x) * side + y},
        "P": {"tp": (x + 1 - 2 * (x % 2)) * side + y},
        "C": {"dp": dp + 1 - 2 * core},
    }

    def remote(src, dst, ssem, rsem, to):
        return pltpu.make_async_remote_copy(
            src_ref=src, dst_ref=dst, send_sem=ssem, recv_sem=rsem, device_id=link[to], device_id_type=MESH
        )

    def sent(ref, sem):
        pltpu.make_async_copy(ref, ref, sem).wait()

    def signal(sem, to):
        pl.semaphore_signal(sem, inc=1, device_id=link[to], device_id_type=MESH)

    barrier = pltpu.get_barrier_semaphore()
    for to in link:
        signal(barrier, to)

    index = {name: i for i, name in enumerate(msgs)}
    kinds = send_kinds(msgs)

    def kind(name):
        return kind_of(msgs[name])

    def source(cls, slot):
        return x_hbm if cls == OWN and slot == 0 else xl.at[cls, slot]

    def gcopy(name):
        to, cls, src, dst, (r, nr), (c, nc) = msgs[name]
        there = OTHER if to == "P" else cls
        block = (pl.ds(r, nr), pl.ds(c, nc))
        return remote(
            source(cls, src).at[block], xl.at[(there, dst, *block)], gsend.at[kinds.index(kind(name))], grecv.at[index[name]], to
        )

    def xload(t, i):
        cls, e, h = tasks[t]
        src = source(cls, TASK_SLOTS[h][i]).at[pl.ds(e * re, re)]
        return pltpu.make_async_copy(src, xbuf.at[t % 2, pl.ds(i * re, re)], xsem.at[t % 2])

    def load_tile(k):
        slot = lax.rem(k, 3)
        cols = pl.ds(pl.multiple_of(lax.rem(k, tiles) * LANES, LANES), LANES)
        return (
            pltpu.make_async_copy(gate_hbm.at[:, cols], gbuf.at[slot, :, pl.ds(0, LANES)], gusem.at[slot]),
            pltpu.make_async_copy(up_hbm.at[:, cols], gbuf.at[slot, :, pl.ds(LANES, LANES)], gusem.at[slot]),
        )

    def wcopy(k):
        there = pl.ds(pl.multiple_of(core * quarter + k * 256, LANES), 256)
        here = pl.ds(pl.multiple_of((1 - role) * half + core * quarter + k * 256, LANES), 256)
        return remote(down_hbm.at[:, here], w.at[pl.ds(width, width), there], wsend, wrecv.at[k], "P")

    def dcopy(k, whose):
        cols = pl.ds(pl.multiple_of(whose * quarter + k * 256, LANES), 256)
        block = w.at[pl.ds(width, width), cols]
        return remote(block, block, dsend, drecv, "C")

    def hcopy(t, i):
        cls, e, h = tasks[t]
        slot = TASK_SLOTS[h][i]
        src = hid.at[(2 * e + 1 - cls) * SLOTS + slot, :, pl.ds(0, width)]
        dst = hid.at[(2 * e + cls) * SLOTS + slot, :, pl.ds(width, width)]
        return remote(src, dst, hsend, hrecv.at[t], "P")

    def do(op):
        kind, what = op[0], op[1]
        if kind == "send":
            gcopy(what).start()
        elif kind == "recv" and what[0] == "W":
            wcopy(what[1]).wait_recv()
        elif kind == "recv":
            gcopy(what).wait_recv()
        elif kind == "load":
            xload(what, op[2]).start()
        elif kind == "wsend":
            wcopy(what).start()
        elif kind == "forward":
            dcopy(what, core).start()
        elif kind == "hsend":
            for i in range(4):
                hcopy(what, i).start()

    def communicate(j):
        for k, (ops, _) in enumerate(steps_):
            if ops:

                @pl.when(j == k)
                def _():
                    for op in ops:
                        do(op)

    def tile(k):
        t, i, slot = k // tiles, lax.rem(k, tiles), lax.rem(k, 3)
        cls, e, h = lax.rem(t // 2, 2), t // 4, lax.rem(t, 2)
        b = lax.rem(t, 2)

        @pl.when(i == 0)
        def _():
            sent(xbuf.at[b], xsem.at[b])

        sent(gbuf.at[slot], gusem.at[slot])

        @pl.when(k + 2 < total_tiles)
        def _():
            for c in load_tile(k + 2):
                c.start()

        acc = jnp.dot(xbuf[b], gbuf[slot], preferred_element_type=jnp.float32)
        gate, up = acc[:, :LANES], acc[:, LANES:]
        h_tile = (jax.nn.silu(gate) * up).astype(hid.dtype)
        cols = pl.ds(pl.multiple_of(i * LANES, LANES), LANES)
        for j in range(4):
            place = TASK_SLOTS[0][j] + h * (TASK_SLOTS[1][j] - TASK_SLOTS[0][j])
            hid[(2 * e + 1 - cls) * SLOTS + place, :, cols] = h_tile[j * re : (j + 1) * re]

    def work(g):
        def one(i, _):
            tile(g * GROUP_TILES + i)
            return 0

        lax.fori_loop(0, GROUP_TILES, one, 0)

    pl.semaphore_wait(barrier, len(link))
    for c in load_tile(0) + load_tile(1):
        c.start()
    load_w = pltpu.make_async_copy(
        down_hbm.at[:, pl.ds(pl.multiple_of(role * half, LANES), half)], w.at[pl.ds(0, width)], wosem
    )
    load_w.start()

    def term(g, slots, start, size):
        out_rows = len(slots) * re
        if slots == tuple(range(slots[0], slots[0] + len(slots))):
            lhs = hid[pl.ds(g * SLOTS + slots[0], len(slots))].reshape(out_rows, 2 * width)
        else:
            lhs = jnp.concatenate([hid[g * SLOTS + s] for s in slots], axis=0)
        return jnp.dot(lhs, w[:, pl.ds(pl.multiple_of(start, LANES), size)], preferred_element_type=jnp.float32)

    f32 = lambda v: v.astype(jnp.float32)
    bf = lambda v: v.astype(jnp.bfloat16)

    def place(s):
        c = lax.rem(s, CHUNKS)
        return s // CHUNKS, c * ncu, 8 * unit + c * ncy, lax.rem(s, NB), lax.rem(s, 2)

    table = (
        ("N", tu1, 0, 0, lu1), ("S", tu1, 0, 1, lu1), ("U", ty1, 1, None, ly1),
        ("N", tu2, 2, 0, lu2), ("S", tu2, 2, 1, lu2), ("N", ty2, 3, 0, ly2), ("S", ty2, 3, 1, ly2),
        ("U", tu3, 4, None, lu3), ("N", ty3, 5, 0, ly3), ("S", ty3, 5, 1, ly3),
    )

    def bcopy(k, s):
        _, _, _, sl, st = place(s)
        to, staging, i, part, landing = table[k]
        src, dst = (staging.at[st], landing.at[sl]) if part is None else (staging.at[st, part], landing.at[sl, part])
        return remote(src, dst, bsend.at[st, i], brecv.at[lax.rem(s, 4), k], to)

    def left(s, k):
        _, staging, i, _, _ = table[k]
        st = lax.rem(s, 2)
        sent(staging.at[st], bsend.at[st, i])

    def free_staging(s, copies):
        @pl.when(s >= 2)
        def _():
            for k in copies:
                left(s - 2, k)

    def arrived(s, kinds):
        for k in kinds:
            bcopy(k, s).wait_recv()

    def stage1(s):
        g, cu, cy, sl, st = place(s)

        @pl.when(lax.rem(s, CHUNKS) == 0)
        def _():
            for h in range(2):
                sent(hid.at[pl.ds(g * SLOTS, 4), :, pl.ds(width, width)], hrecv.at[2 * g + h])

        free_staging(s, (0, 2))
        t = term(g, (4, 5), cu, ncu).reshape(2, re, ncu)
        tu1[st, 0] = bf(t[:, :hr])
        tu1[st, 1] = bf(t[:, hr:])
        for k in (0, 1):
            bcopy(k, s).start()
        t = term(g, (1, 3, 5, 7), cy, ncy)
        ty1[st] = bf(t).reshape(4, re, ncy)
        bcopy(2, s).start()

    def stage2(s):
        g, cu, cy, sl, st = place(s)
        arrived(s, (0, 1, 2))
        free_staging(s, (3, 5))
        t = term(g, (2, 3), cu, ncu).reshape(2, re, ncu)
        tu2[st, 0, :, :hr] = bf(t[:, :hr] + f32(lu1[sl, 0]))
        tu2[st, 0, :, hr:] = bf(t[:, hr:])
        bcopy(3, s).start()
        t = term(g, (6, 7), cu, ncu).reshape(2, re, ncu)
        tu2[st, 1, :, :hr] = bf(t[:, :hr])
        tu2[st, 1, :, hr:] = bf(t[:, hr:] + f32(lu1[sl, 1]))
        bcopy(4, s).start()
        t = term(g, (4,), cy, ncy) + f32(ly1[sl, 2])
        ty2[st, 0] = bf(t[:hr])
        ty2[st, 1] = bf(t[hr:])
        for k in (5, 6):
            bcopy(k, s).start()

    def stage3(s):
        g, cu, cy, sl, st = place(s)
        arrived(s, (3, 4, 5, 6))
        free_staging(s, (7, 8))
        t = term(g, (1,), cu, ncu)
        tu3[st] = bf(t + f32(lu2[sl, 0, 1]) + f32(lu2[sl, 1, 1]))
        bcopy(7, s).start()
        t = term(g, (2,), cy, ncy) + f32(ly1[sl, 1])
        ty3[st, 0, :hr] = bf(t[:hr] + f32(ly2[sl, 0]))
        ty3[st, 0, hr:] = bf(t[hr:])
        t = term(g, (6,), cy, ncy) + f32(ly1[sl, 3])
        ty3[st, 1, :hr] = bf(t[:hr])
        ty3[st, 1, hr:] = bf(t[hr:] + f32(ly2[sl, 1]))
        for k in (8, 9):
            bcopy(k, s).start()

    def fcopy(s, k):
        g, cu, cy, _, st = place(s)
        start, size = ((cu, ncu), (cy, ncy))[k]
        r = pl.ds(pl.multiple_of((g // 2) * re, 8), re)
        cols = pl.ds(pl.multiple_of(role * half + start, LANES), size)
        c = lax.rem(s, CHUNKS)
        return remote(tq.at[c, :, pl.ds(k * ncu, size)], out.at[r, cols], fsend.at[c], frecv.at[g // 2], "P")

    def stage4(s):
        g, cu, cy, sl, st = place(s)
        e, c = g // 2, lax.rem(s, CHUNKS)
        arrived(s, (7, 8, 9))

        @pl.when(lax.rem(g, 2) == 0)
        def _():
            @pl.when(e > 0)
            def _():
                sent(tq.at[c], fsend.at[c])

        tu = term(g, (0,), cu, ncu) + f32(lu2[sl, 0, 0]) + f32(lu2[sl, 1, 0]) + f32(lu3[sl])
        ty = term(g, (0,), cy, ncy) + f32(ly1[sl, 0]) + f32(ly3[sl, 0]) + f32(ly3[sl, 1])

        @pl.when(lax.rem(g, 2) == 0)
        def _():
            tq[c, :, pl.ds(0, ncu)] = bf(tu)
            tq[c, :, pl.ds(ncu, ncy)] = bf(ty)
            for k in range(2):
                fcopy(s, k).start()

        @pl.when(lax.rem(g, 2) == 1)
        def _():
            r = pl.ds(pl.multiple_of(e * re, 8), re)
            out[r, pl.ds(pl.multiple_of(role * half + cu, LANES), ncu)] = bf(tu)
            out[r, pl.ds(pl.multiple_of(role * half + cy, LANES), ncy)] = bf(ty)

    def reduce_step(i):
        @pl.when(i == 0)
        def _():
            sent(w.at[pl.ds(0, width), pl.ds(0, quarter)], drecv)
            load_w.wait()

        @pl.when(i == steps)
        def _():
            for k, (_, r, (_, c)) in enumerate(kinds):
                blocks = sum(kind(name) == kinds[k] for name in msgs) * r // rows
                sent(xl.at[OWN, pl.ds(0, blocks), :, pl.ds(0, c)], gsend.at[k])
            sent(w.at[pl.ds(0, width), pl.ds(0, quarter)], wsend)
            sent(w.at[pl.ds(0, width), pl.ds(0, quarter)], dsend)
            sent(hid.at[:, :, pl.ds(0, width)], hsend)

        for lag, stage in ((3 * LAG, stage4), (2 * LAG, stage3), (LAG, stage2), (0, stage1)):

            @pl.when((i >= lag) & (i < steps + lag))
            def _():
                stage(i - lag)

    reductions = [k for k, (_, kind) in enumerate(steps_) if kind == "B"]

    def body(j, _):
        communicate(j)
        before, here = jnp.int32(0), jnp.int32(0)
        for k in reductions:
            before += (j > k).astype(jnp.int32)
            here += (j == k).astype(jnp.int32)

        @pl.when(here == 0)
        def _():
            work(j - before)

        @pl.when(here == 1)
        def _():
            reduce_step(before)

        return 0

    lax.fori_loop(0, len(steps_) - 1, body, 0)
    for op in steps_[-1][0]:
        do(op)

    for e in range(EPOCHS):
        sent(out.at[pl.ds(0, re), pl.ds(0, half)], frecv.at[e])
    for s in (steps - 2, steps - 1):
        for k in (0, 2, 3, 5, 7, 8):
            left(s, k)
    for c in range(CHUNKS):
        sent(tq.at[c], fsend.at[c])


def solution(mesh):
    n = mesh.shape["tp"]

    def step(x, w_gate, w_up, w_down):
        (rows, depth), width = x.shape, w_gate.shape[1]
        order = plan(depth, rows, width)
        msgs = gather_messages(depth, rows)[0]
        re, half = rows // EPOCHS, depth // 2
        hr, unit = re // 2, depth // 28
        ncu, ncy = 8 * unit // CHUNKS, 6 * unit // CHUNKS
        pieces = half // 2 // 256
        tasks = 4 * EPOCHS
        pieces_of_sums = (2, 2, hr, ncu), (2, 2, re, ncu), (re, ncu), (4, re, ncy), (2, hr, ncy), (2, re, ncy)
        vmem = lambda *shape: pltpu.VMEM(shape, x.dtype)
        dma = lambda *shape: pltpu.SemaphoreType.DMA(shape)
        return pl.pallas_call(
            functools.partial(kernel, n, order, msgs),
            out_shape=(pltpu.VMEM(x.shape, x.dtype), jax.ShapeDtypeStruct((2, SLOTS, rows, depth), x.dtype)),
            in_specs=[pl.BlockSpec(memory_space=pl.ANY)] * 4,
            out_specs=(pl.BlockSpec(memory_space=pltpu.VMEM), pl.BlockSpec(memory_space=pl.ANY)),
            scratch_shapes=[
                vmem(3, depth, 2 * LANES),
                vmem(2 * width, half),
                vmem(2, 4 * re, depth),
                vmem(2 * EPOCHS * SLOTS, re, 2 * width),
                *(vmem(NB, *p) for p in pieces_of_sums),
                *(vmem(2, *p) for p in pieces_of_sums),
                vmem(CHUNKS, re, ncu + ncy),
                dma(len(send_kinds(msgs))),
                dma(len(msgs)),
                dma(2),
                dma(3),
                pltpu.SemaphoreType.DMA,
                pltpu.SemaphoreType.DMA,
                dma(pieces),
                pltpu.SemaphoreType.DMA,
                pltpu.SemaphoreType.DMA,
                pltpu.SemaphoreType.DMA,
                dma(tasks),
                dma(2, 6),
                dma(4, 10),
                dma(CHUNKS),
                dma(EPOCHS),
            ],
            compiler_params=pltpu.CompilerParams(
                collective_id=0, has_side_effects=True, vmem_limit_bytes=VLIM
            ),
        )(x, w_gate, w_up, w_down)[0]

    return jax.shard_map(
        step,
        mesh=mesh,
        in_specs=(P(("dp", "tp"), None), P(None, "tp"), P(None, "tp"), P("tp", None)),
        out_specs=P(("dp", "tp"), None),
        check_vma=False,
    )
```

time: 602 us -> 356 us (0.59)
  waiting for transfers between devices: 419 us -> 0 us
  Pallas kernels: 0 us -> 355 us
  matrix products: 169 us -> 0 us
  between operations: 13.4 us -> 0.01 us
    pallas_call x0 -> x1, Pallas kernels: none -> 355 us  [step(): pl.pallas_call(functools.partial(kernel, n, order, msgs), out_shape=(pltp...]
    all_gather x1 -> x0, waiting for transfers between devices: 212 us -> none  [step(): rows = lax.all_gather(x, 'tp', axis=0, tiled=True)]
    reduce_scatter x1 -> x0, waiting for transfers between devices: 205 us -> none  [step(): return lax.psum_scatter(term, 'tp', scatter_dimension=0, tiled=True)]
    dot_general x3 -> x0, matrix products: 169 us -> none  [the longest x1 57.3 us: step(): gate = jnp.dot(rows, w_gate, preferred_element_type=jnp.float32)]
  transfers between devices with their start and end apart: 2 -> 0, of which waited for: 2 -> 0; matrix products, arithmetic and copies ran while one was open for 0% -> 0% of each run, Pallas kernels for 0% -> 0%
where the time goes in v1:
time: 356 us
  Pallas kernels  355 us (100%)
    pallas_call x1, Pallas kernels, step(): pl.pallas_call(functools.partial(kernel, n, order, msgs), out_shape=(pltp...  355 us

profile of v1, /device:TPU:96, one launch (start us, length us, event | category | flops | bytes accessed | tf_op | source)
XLA Modules:
  0.0 355.9 jit_solution(11730748485692441284)
XLA Ops:
  0.0 354.5 %shard_map.46 = (bf16[160,7168]{1,0:T(8,128)(2,1)S(1)}, bf16[2,8,160,7168]{3,2,1,0:T(8,128)(2,1)}) custom-call(bf16[160,7168]{1,0:T(8,128)(2,1)} %x_hbm.1, bf16[7168,1152]{1,0:T(8,128)(2,1)} %gate_hbm.1, bf16[7168,1152]{1,0:T(8,128)(2,1)} %up_hbm.1, bf16[1152,7168]{1,0:T(8,128)(2,1)} %down_hbm.1), custom_call_target="tpu_custom_call" | custom-call | tf_op jit(solution)/shard_map/pallas_call | solution.py:593
  354.5 1.4 copy.6

commit v2 on v1

--- a/solution.py
+++ b/solution.py
@@ -12,17 +12,18 @@
 LANES = 128
 EPOCHS = 2
 OWN, OTHER = 0, 1
-SLOTS = 8
 TASK_SLOTS = ((0, 1, 2, 6), (3, 7, 4, 5))
 GROUP_TILES = 3
 LAG = 2
-NB = 8
+NB = 10
+FLAGS = 6
 CHUNKS = 4
+BATCHES, STAGE_US = (range(3), range(3, 7), range(7, 10)), (1.62, 1.73, 1.2, 0.98)
 VLIM = 64600000
 
 
 FIRST_U, BY_PARTNER = (14, 17), 2
-TUNE = {'due_w': (95, 74), 'due_f': (70, 240), 'due_p': 815, 'due_h': (790, -30, 410, -30, 570, -170, 190, -130), 'backlog': 32.0, 'prefer': 438, 'phase': (1, 3, 3, 0.5)}
+TUNE = {'due_w': (195, 100), 'due_f': (-1230, 1770), 'due_p': 3555, 'due_h': (-5230, -2790, 1010, 7030, 5030, 8890, 8690, 6690), 'backlog': 32, 'prefer': 26, 'phase': (0, 1.5, 3, 2.5)}
 
 
 def columns(depth):
@@ -86,7 +87,7 @@
 
 
 def plan(depth, rows, width):
-    rate, delay, tile_us, gt = 46.6e3, 2.2, 1.46, GROUP_TILES
+    rate, delay, tile_us, gt = 46.6e3, 2.3, 1.48, GROUP_TILES
     due_w, due_f, due_p, due_h, backlog = (TUNE[k] for k in ("due_w", "due_f", "due_p", "due_h", "backlog"))
     msgs, deps = gather_messages(depth, rows)
     pending = {name: set(d) for name, d in deps.items()}
@@ -114,12 +115,10 @@
         copies["W", k] = ("P", width * 256 * 2, due_w[0] + due_w[1] * k)
     for t in range(len(tasks)):
         copies["H", t] = ("P", 4 * re * width * 2, due_h[t] + 10 * t)
-    parts = {
-        0: ("N", re * ncu), 1: ("S", re * ncu), 2: ("U", 4 * re * ncy),
-        3: ("N", 2 * re * ncu), 4: ("S", 2 * re * ncu), 5: ("N", re // 2 * ncy), 6: ("S", re // 2 * ncy),
-        7: ("U", re * ncu), 8: ("N", re * ncy), 9: ("S", re * ncy),
-    }
-    stages = (((0, 1, 2), 1.65, ()), ((3, 4, 5, 6), 1.75, (0, 1, 2)), ((7, 8, 9), 1.35, (3, 4, 5, 6)), ((), 1.0, (7, 8, 9)))
+    u, y = re * ncu, re * ncy
+    parts = (
+        ("N", u), ("S", u), ("U", 4 * y), ("N", 2 * u), ("S", 2 * u), ("N", y // 2), ("S", y // 2), ("U", u), ("N", y), ("S", y),
+    )
     free = dict.fromkeys("NSUPC", 0.0)
     avail = [n for n in msgs if not pending[n]] + [("W", k) for k in range(pieces)]
     now, arrivals = 0.0, []
@@ -131,8 +130,8 @@
     def emit(*op):
         ops.append(op)
 
-    def post(link, nbytes, what, at=None):
-        free[link] = max(now if at is None else at, free[link]) + nbytes / (rate if link != "C" else 300e3)
+    def post(link, nbytes, what):
+        free[link] = max(now, free[link]) + nbytes / (rate if link != "C" else 300e3)
         arrived[what] = free[link] + delay
         if what[0] not in "DHBE":
             arrivals.append((free[link] + delay, what))
@@ -153,23 +152,25 @@
 
     INF = 1e9
 
+    def waits(j):
+        return BATCHES[j - 1] if j else ()
+
+    def active():
+        return [(j, it - j * LAG) for j in range(4) if 0 <= it - j * LAG < nsteps]
+
     def b_ready():
-        t = 0.0
-        if it < nsteps:
+        t, offset = 0.0, 0.0
+        if it < nsteps and it % CHUNKS == 0:
             g = it // CHUNKS
-            if it % CHUNKS == 0:
-                e, cls = g // 2, 1 - g % 2
-                if task <= e * 4 + cls * 2 + 1 or forwarded < pieces:
-                    return INF
-                for k in range(2):
-                    t = max(t, arrived.get(("H", 2 * g + k), INF))
+            e, cls = g // 2, 1 - g % 2
+            if task <= e * 4 + cls * 2 + 1 or forwarded < pieces:
+                return INF
+            t = max(arrived.get(("H", 2 * g + k), INF) for k in range(2))
             if it == 0:
                 t = max(t, max(arrived["D", k] for k in range(pieces)))
-        for j in (1, 2, 3):
-            s = it - j * LAG
-            if 0 <= s < nsteps:
-                for k in stages[j][2]:
-                    t = max(t, arrived["B", k, s])
+        for j, s in active():
+            t = max([t] + [arrived.get(("B", k, s), now + 5) - offset for k in waits(j)])
+            offset += STAGE_US[j]
         return t
 
     while task < len(tasks) or it < nsteps + 3 * LAG:
@@ -198,8 +199,7 @@
         b_at = b_ready() if it < nsteps + 3 * LAG else INF
         choice = None
         if b_at <= now and tile_at <= now:
-            busy = min(free["N"], free["U"]) - now
-            choice = "B" if busy < TUNE["prefer"] else "T"
+            choice = "B" if min(free["N"], free["U"]) - now < TUNE["prefer"] else "T"
         elif b_at <= now:
             choice = "B"
         elif tile_at <= now:
@@ -216,19 +216,17 @@
         if choice == "B":
             steps.append((ops, "B"))
             ops = []
-            for j in (3, 2, 1, 0):
-                s = it - j * LAG
-                if 0 <= s < nsteps:
-                    now += stages[j][1]
-                    for k in stages[j][0]:
-                        link, n = parts[k]
-                        post(link, 2 * n, ("B", k, s))
-                    if j == 3 and s // CHUNKS % 2 == 0:
-                        post("P", 2 * re * (ncu + ncy), ("E", s))
+            for j, s in active():
+                now = max([now] + [arrived["B", k, s] for k in waits(j)]) + STAGE_US[j]
+                for k in BATCHES[j] if j < len(BATCHES) else ():
+                    link, n = parts[k]
+                    post(link, 2 * n, ("B", k, s))
+                if j == 3 and s // CHUNKS in (1, 2):
+                    post("P", 2 * re * (ncu + ncy), ("E", s))
             now += 0.1
             it += 1
             continue
-        times = [a[0] for a in arrivals] + [t for t in (tile_at, b_at) if t < INF]
+        times = [a[0] for a in arrivals] + [t for t in (tile_at, b_at) if now < t < INF]
         if avail:
             times.append(min(max(now + 0.3, free[copies[n][0]] - backlog + 0.1) for n in avail))
         now = max(now, min(times))
@@ -242,6 +240,7 @@
            gsend, grecv, xsem, gusem, wosem, wsend, wrecv, dsend, drecv, hsend, hrecv,
            bsend, brecv, fsend, frecv):
     rows, depth = x_hbm.shape
+    slots = n // 2
     width = gate_hbm.shape[1]
     re, half = rows // EPOCHS, depth // 2
     quarter, hr = half // 2, re // 2
@@ -323,8 +322,8 @@
     def hcopy(t, i):
         cls, e, h = tasks[t]
         slot = TASK_SLOTS[h][i]
-        src = hid.at[(2 * e + 1 - cls) * SLOTS + slot, :, pl.ds(0, width)]
-        dst = hid.at[(2 * e + cls) * SLOTS + slot, :, pl.ds(width, width)]
+        src = hid.at[(2 * e + 1 - cls) * slots + slot, :, pl.ds(0, width)]
+        dst = hid.at[(2 * e + cls) * slots + slot, :, pl.ds(width, width)]
         return remote(src, dst, hsend, hrecv.at[t], "P")
 
     def do(op):
@@ -376,7 +375,7 @@
         cols = pl.ds(pl.multiple_of(i * LANES, LANES), LANES)
         for j in range(4):
             place = TASK_SLOTS[0][j] + h * (TASK_SLOTS[1][j] - TASK_SLOTS[0][j])
-            hid[(2 * e + 1 - cls) * SLOTS + place, :, cols] = h_tile[j * re : (j + 1) * re]
+            hid[(2 * e + 1 - cls) * slots + place, :, cols] = h_tile[j * re : (j + 1) * re]
 
     def work(g):
         def one(i, _):
@@ -393,12 +392,11 @@
     )
     load_w.start()
 
-    def term(g, slots, start, size):
-        out_rows = len(slots) * re
-        if slots == tuple(range(slots[0], slots[0] + len(slots))):
-            lhs = hid[pl.ds(g * SLOTS + slots[0], len(slots))].reshape(out_rows, 2 * width)
+    def term(g, which, start, size):
+        if which == tuple(range(which[0], which[0] + len(which))):
+            lhs = hid[pl.ds(g * slots + which[0], len(which))].reshape(len(which) * re, 2 * width)
         else:
-            lhs = jnp.concatenate([hid[g * SLOTS + s] for s in slots], axis=0)
+            lhs = jnp.concatenate([hid[g * slots + s] for s in which], axis=0)
         return jnp.dot(lhs, w[:, pl.ds(pl.multiple_of(start, LANES), size)], preferred_element_type=jnp.float32)
 
     f32 = lambda v: v.astype(jnp.float32)
@@ -418,7 +416,7 @@
         _, _, _, sl, st = place(s)
         to, staging, i, part, landing = table[k]
         src, dst = (staging.at[st], landing.at[sl]) if part is None else (staging.at[st, part], landing.at[sl, part])
-        return remote(src, dst, bsend.at[st, i], brecv.at[lax.rem(s, 4), k], to)
+        return remote(src, dst, bsend.at[st, i], brecv.at[lax.rem(s, FLAGS), table[k][2] // 2], to)
 
     def left(s, k):
         _, staging, i, _, _ = table[k]
@@ -431,9 +429,9 @@
             for k in copies:
                 left(s - 2, k)
 
-    def arrived(s, kinds):
-        for k in kinds:
-            bcopy(k, s).wait_recv()
+    def arrived(s, batch):
+        words = sum(math.prod(table[k][4].shape[1 if table[k][3] is None else 2 :]) for k in BATCHES[batch])
+        sent(w.at[pl.ds(0, words // 256), pl.ds(0, 256)], brecv.at[lax.rem(s, FLAGS), batch])
 
     def stage1(s):
         g, cu, cy, sl, st = place(s)
@@ -441,7 +439,7 @@
         @pl.when(lax.rem(s, CHUNKS) == 0)
         def _():
             for h in range(2):
-                sent(hid.at[pl.ds(g * SLOTS, 4), :, pl.ds(width, width)], hrecv.at[2 * g + h])
+                sent(hid.at[pl.ds(g * slots, 4), :, pl.ds(width, width)], hrecv.at[2 * g + h])
 
         free_staging(s, (0, 2))
         t = term(g, (4, 5), cu, ncu).reshape(2, re, ncu)
@@ -455,7 +453,7 @@
 
     def stage2(s):
         g, cu, cy, sl, st = place(s)
-        arrived(s, (0, 1, 2))
+        arrived(s, 0)
         free_staging(s, (3, 5))
         t = term(g, (2, 3), cu, ncu).reshape(2, re, ncu)
         tu2[st, 0, :, :hr] = bf(t[:, :hr] + f32(lu1[sl, 0]))
@@ -473,17 +471,17 @@
 
     def stage3(s):
         g, cu, cy, sl, st = place(s)
-        arrived(s, (3, 4, 5, 6))
+        arrived(s, 1)
         free_staging(s, (7, 8))
         t = term(g, (1,), cu, ncu)
         tu3[st] = bf(t + f32(lu2[sl, 0, 1]) + f32(lu2[sl, 1, 1]))
         bcopy(7, s).start()
-        t = term(g, (2,), cy, ncy) + f32(ly1[sl, 1])
-        ty3[st, 0, :hr] = bf(t[:hr] + f32(ly2[sl, 0]))
-        ty3[st, 0, hr:] = bf(t[hr:])
-        t = term(g, (6,), cy, ncy) + f32(ly1[sl, 3])
-        ty3[st, 1, :hr] = bf(t[:hr])
-        ty3[st, 1, hr:] = bf(t[hr:] + f32(ly2[sl, 1]))
+        t = term(g, (2, 6), cy, ncy)
+        a, b = t[:re] + f32(ly1[sl, 1]), t[re:] + f32(ly1[sl, 3])
+        ty3[st, 0, :hr] = bf(a[:hr] + f32(ly2[sl, 0]))
+        ty3[st, 0, hr:] = bf(a[hr:])
+        ty3[st, 1, :hr] = bf(b[:hr])
+        ty3[st, 1, hr:] = bf(b[hr:] + f32(ly2[sl, 1]))
         for k in (8, 9):
             bcopy(k, s).start()
 
@@ -498,7 +496,7 @@
     def stage4(s):
         g, cu, cy, sl, st = place(s)
         e, c = g // 2, lax.rem(s, CHUNKS)
-        arrived(s, (7, 8, 9))
+        arrived(s, 2)
 
         @pl.when(lax.rem(g, 2) == 0)
         def _():
@@ -513,8 +511,11 @@
         def _():
             tq[c, :, pl.ds(0, ncu)] = bf(tu)
             tq[c, :, pl.ds(ncu, ncy)] = bf(ty)
+
+        @pl.when((g == 1) | (g == 2))
+        def _():
             for k in range(2):
-                fcopy(s, k).start()
+                fcopy(s - CHUNKS * (2 - g), k).start()
 
         @pl.when(lax.rem(g, 2) == 1)
         def _():
@@ -537,7 +538,7 @@
             sent(w.at[pl.ds(0, width), pl.ds(0, quarter)], dsend)
             sent(hid.at[:, :, pl.ds(0, width)], hsend)
 
-        for lag, stage in ((3 * LAG, stage4), (2 * LAG, stage3), (LAG, stage2), (0, stage1)):
+        for lag, stage in ((0, stage1), (LAG, stage2), (2 * LAG, stage3), (3 * LAG, stage4)):
 
             @pl.when((i >= lag) & (i < steps + lag))
             def _():
@@ -592,14 +593,14 @@
         dma = lambda *shape: pltpu.SemaphoreType.DMA(shape)
         return pl.pallas_call(
             functools.partial(kernel, n, order, msgs),
-            out_shape=(pltpu.VMEM(x.shape, x.dtype), jax.ShapeDtypeStruct((2, SLOTS, rows, depth), x.dtype)),
+            out_shape=(pltpu.VMEM(x.shape, x.dtype), jax.ShapeDtypeStruct((2, n // 2, rows, depth), x.dtype)),
             in_specs=[pl.BlockSpec(memory_space=pl.ANY)] * 4,
             out_specs=(pl.BlockSpec(memory_space=pltpu.VMEM), pl.BlockSpec(memory_space=pl.ANY)),
             scratch_shapes=[
                 vmem(3, depth, 2 * LANES),
                 vmem(2 * width, half),
                 vmem(2, 4 * re, depth),
-                vmem(2 * EPOCHS * SLOTS, re, 2 * width),
+                vmem(EPOCHS * n, re, 2 * width),
                 *(vmem(NB, *p) for p in pieces_of_sums),
                 *(vmem(2, *p) for p in pieces_of_sums),
                 vmem(CHUNKS, re, ncu + ncy),
@@ -615,7 +616,7 @@
                 pltpu.SemaphoreType.DMA,
                 dma(tasks),
                 dma(2, 6),
-                dma(4, 10),
+                dma(FLAGS, 3),
                 dma(CHUNKS),
                 dma(EPOCHS),
             ],

time: 356 us -> 353 us (level)
  Pallas kernels: 355 us -> 351 us
    pallas_call x1, Pallas kernels: 355 us -> 351 us  [step(): pl.pallas_call(functools.partial(kernel, n, order, msgs), out_shape=(pltp...]
where the time goes in v2:
time: 353 us; the launch traced here: 352 us
  Pallas kernels  351 us (99%)
    pallas_call x1, Pallas kernels, step(): pl.pallas_call(functools.partial(kernel, n, order, msgs), out_shape=(pltp...  351 us

profile of v2, /device:TPU:96, one launch (start us, length us, event | category | flops | bytes accessed | tf_op | source)
XLA Modules:
  0.0 352.3 jit_solution(8664089178819043994)
XLA Ops:
  0.0 350.9 %shard_map.46 = (bf16[160,7168]{1,0:T(8,128)(2,1)S(1)}, bf16[2,8,160,7168]{3,2,1,0:T(8,128)(2,1)}) custom-call(bf16[160,7168]{1,0:T(8,128)(2,1)} %x_hbm.1, bf16[7168,1152]{1,0:T(8,128)(2,1)} %gate_hbm.1, bf16[7168,1152]{1,0:T(8,128)(2,1)} %up_hbm.1, bf16[1152,7168]{1,0:T(8,128)(2,1)} %down_hbm.1), custom_call_target="tpu_custom_call" | custom-call | tf_op jit(solution)/shard_map/pallas_call | solution.py:594
  350.9 1.4 copy.6

commit v3 on v2

--- a/solution.py
+++ b/solution.py
@@ -12,25 +12,29 @@
 LANES = 128
 EPOCHS = 2
 OWN, OTHER = 0, 1
-TASK_SLOTS = ((0, 1, 2, 6), (3, 7, 4, 5))
+TASK_SLOTS = (0, 1, 2, 6), (3, 7, 4, 5)
+PARTS = ((1,), (2, 6), (0,)), ((3, 7, 4, 5),)
 GROUP_TILES = 3
-LAG = 2
 NB = 10
-FLAGS = 6
+FLAGS = 7
 CHUNKS = 4
-BATCHES, STAGE_US = (range(3), range(3, 7), range(7, 10)), (1.62, 1.73, 1.2, 0.98)
+LAGS = (0, 1, 3, 6), (0, 2, 4, 6)
+STAGE_US = (0.6, 1.0, 0.57, 0.61), (0.98, 0.48, 0.61, 0.52)
+LINKS = ("NS", "NS", "U"), ("U", "NS", "NS")
+SHARE = (1, 2, 1), (4, 0.5, 1)
+STAGES = [(i, j) for j in range(4) for i in range(2)]
 VLIM = 64600000
 
 
-FIRST_U, BY_PARTNER = (14, 17), 2
-TUNE = {'due_w': (195, 100), 'due_f': (-1230, 1770), 'due_p': 3555, 'due_h': (-5230, -2790, 1010, 7030, 5030, 8890, 8690, 6690), 'backlog': 32, 'prefer': 26, 'phase': (0, 1.5, 3, 2.5)}
+FIRST_U, BY_PARTNER = (28, 31), 6
+TUNE = {'due_w': (-2320, 691), 'due_f': (-3850, 1390), 'due_p': 1165, 'due_h': (-390, -1270, -4350, 1830, 870, 12450, 10410, 15370), 'backlog': 6, 'prefer': 48, 'phase': (1, 1, 3, 3), 'hb': 3110, 'blp': 10}
 
 
 def columns(depth):
-    t, (own, other) = depth // 28, FIRST_U
-    end = 28 - BY_PARTNER
+    t, (own, other) = depth // 56, FIRST_U
+    end = 56 - BY_PARTNER
     return {
-        OWN: ((0, own * t), (own * t, (28 - own) * t), None),
+        OWN: ((0, own * t), (own * t, (56 - own) * t), None),
         OTHER: ((0, other * t), (other * t, (end - other) * t), (end * t, BY_PARTNER * t)),
     }
 
@@ -114,11 +118,9 @@
     for k in range(pieces):
         copies["W", k] = ("P", width * 256 * 2, due_w[0] + due_w[1] * k)
     for t in range(len(tasks)):
-        copies["H", t] = ("P", 4 * re * width * 2, due_h[t] + 10 * t)
-    u, y = re * ncu, re * ncy
-    parts = (
-        ("N", u), ("S", u), ("U", 4 * y), ("N", 2 * u), ("S", 2 * u), ("N", y // 2), ("S", y // 2), ("U", u), ("N", y), ("S", y),
-    )
+        for part, slots in enumerate(PARTS[t % 2]):
+            due = due_h[t + 1] + 10 * t + 11 + part + TUNE["hb"] if part else due_h[t] + 10 * t
+            copies["H", t, part] = ("P", len(slots) * re * width * 2, due)
     free = dict.fromkeys("NSUPC", 0.0)
     avail = [n for n in msgs if not pending[n]] + [("W", k) for k in range(pieces)]
     now, arrivals = 0.0, []
@@ -139,9 +141,9 @@
     def issue():
         for n in sorted(avail, key=lambda n: copies[n][2]):
             link, nbytes, _ = copies[n]
-            if free[link] - now < backlog:
+            if free[link] - now < (TUNE["blp"] if link == "P" else backlog):
                 avail.remove(n)
-                emit({"W": "wsend", "H": "hsend"}.get(n[0], "send"), n[1] if n[0] in "WH" else n)
+                emit(*(("wsend", n[1]) if n[0] == "W" else ("hsend", *n[1:]) if n[0] == "H" else ("send", n)))
                 post(link, nbytes, n)
         for k in range(task, min(task + 2, len(tasks))):
             cls, e, h = tasks[k]
@@ -152,11 +154,11 @@
 
     INF = 1e9
 
-    def waits(j):
-        return BATCHES[j - 1] if j else ()
-
     def active():
-        return [(j, it - j * LAG) for j in range(4) if 0 <= it - j * LAG < nsteps]
+        return [(i, j, it - LAGS[i][j]) for i, j in STAGES if 0 <= it - LAGS[i][j] < nsteps]
+
+    def waits(i, j):
+        return [("B", i, j - 1, part) for part in range(len(LINKS[i][j - 1]))] if j else []
 
     def b_ready():
         t, offset = 0.0, 0.0
@@ -165,15 +167,15 @@
             e, cls = g // 2, 1 - g % 2
             if task <= e * 4 + cls * 2 + 1 or forwarded < pieces:
                 return INF
-            t = max(arrived.get(("H", 2 * g + k), INF) for k in range(2))
+            t = max(arrived.get(("H", 2 * g + k, 0), INF) for k in range(2))
             if it == 0:
                 t = max(t, max(arrived["D", k] for k in range(pieces)))
-        for j, s in active():
-            t = max([t] + [arrived.get(("B", k, s), now + 5) - offset for k in waits(j)])
-            offset += STAGE_US[j]
+        for i, j, s in active():
+            t = max([t] + [arrived.get((*q, s), now + 5) - offset for q in waits(i, j)])
+            offset += STAGE_US[i][j]
         return t
 
-    while task < len(tasks) or it < nsteps + 3 * LAG:
+    while task < len(tasks) or it < nsteps + LAGS[1][3]:
         issue()
         for a in sorted((a for a in arrivals if a[0] <= now), key=lambda a: a[0]):
             arrivals.remove(a)
@@ -196,7 +198,7 @@
         tile_at = INF
         if task < len(tasks) and all((task, i) in loaded for i in range(4)):
             tile_at = max(loaded[task, i] for i in range(4))
-        b_at = b_ready() if it < nsteps + 3 * LAG else INF
+        b_at = b_ready() if it < nsteps + LAGS[1][3] else INF
         choice = None
         if b_at <= now and tile_at <= now:
             choice = "B" if min(free["N"], free["U"]) - now < TUNE["prefer"] else "T"
@@ -210,25 +212,27 @@
             now += gt * tile_us
             sub += 1
             if sub == subs:
-                avail.append(("H", task))
+                avail.extend(("H", task, part) for part in range(len(PARTS[task % 2])))
                 task, sub = task + 1, 0
             continue
         if choice == "B":
             steps.append((ops, "B"))
             ops = []
-            for j, s in active():
-                now = max([now] + [arrived["B", k, s] for k in waits(j)]) + STAGE_US[j]
-                for k in BATCHES[j] if j < len(BATCHES) else ():
-                    link, n = parts[k]
-                    post(link, 2 * n, ("B", k, s))
+            for i, j, s in active():
+                need = [(*q, s) for q in waits(i, j)]
+                if s % CHUNKS == 0 and (i, j) in ((0, 1), (0, 3)):
+                    need.append(("H", 2 * (s // CHUNKS), 1 if j == 1 else 2))
+                now = max([now] + [arrived[q] for q in need]) + STAGE_US[i][j]
+                for part, to in enumerate(LINKS[i][j] if j < 3 else ""):
+                    post(to, 2 * SHARE[i][j] * re * (ncu, ncy)[i], ("B", i, j, part, s))
                 if j == 3 and s // CHUNKS in (1, 2):
-                    post("P", 2 * re * (ncu + ncy), ("E", s))
-            now += 0.1
+                    post("P", 2 * re * (ncu, ncy)[i], ("E", i, s))
+            now += 0.3
             it += 1
             continue
         times = [a[0] for a in arrivals] + [t for t in (tile_at, b_at) if now < t < INF]
         if avail:
-            times.append(min(max(now + 0.3, free[copies[n][0]] - backlog + 0.1) for n in avail))
+            times.append(min(max(now + 0.3, free[copies[n][0]] - (TUNE["blp"] if copies[n][0] == "P" else backlog) + 0.1) for n in avail))
         now = max(now, min(times))
     assert not avail and not arrivals, (avail, arrivals)
     steps.append((ops, ""))
@@ -319,12 +323,11 @@
         block = w.at[pl.ds(width, width), cols]
         return remote(block, block, dsend, drecv, "C")
 
-    def hcopy(t, i):
-        cls, e, h = tasks[t]
-        slot = TASK_SLOTS[h][i]
+    def hcopy(t, part, slot):
+        cls, e, _ = tasks[t]
         src = hid.at[(2 * e + 1 - cls) * slots + slot, :, pl.ds(0, width)]
         dst = hid.at[(2 * e + cls) * slots + slot, :, pl.ds(width, width)]
-        return remote(src, dst, hsend, hrecv.at[t], "P")
+        return remote(src, dst, hsend, hrecv.at[t, part], "P")
 
     def do(op):
         kind, what = op[0], op[1]
@@ -341,8 +344,8 @@
         elif kind == "forward":
             dcopy(what, core).start()
         elif kind == "hsend":
-            for i in range(4):
-                hcopy(what, i).start()
+            for slot in PARTS[what % 2][op[2]]:
+                hcopy(what, op[2], slot).start()
 
     def communicate(j):
         for k, (ops, _) in enumerate(steps_):
@@ -406,84 +409,105 @@
         c = lax.rem(s, CHUNKS)
         return s // CHUNKS, c * ncu, 8 * unit + c * ncy, lax.rem(s, NB), lax.rem(s, 2)
 
-    table = (
-        ("N", tu1, 0, 0, lu1), ("S", tu1, 0, 1, lu1), ("U", ty1, 1, None, ly1),
-        ("N", tu2, 2, 0, lu2), ("S", tu2, 2, 1, lu2), ("N", ty2, 3, 0, ly2), ("S", ty2, 3, 1, ly2),
-        ("U", tu3, 4, None, lu3), ("N", ty3, 5, 0, ly3), ("S", ty3, 5, 1, ly3),
-    )
-
-    def bcopy(k, s):
+    staging, landing = ((tu1, tu2, tu3), (ty1, ty2, ty3)), ((lu1, lu2, lu3), (ly1, ly2, ly3))
+
+    def send(s, i, j):
         _, _, _, sl, st = place(s)
-        to, staging, i, part, landing = table[k]
-        src, dst = (staging.at[st], landing.at[sl]) if part is None else (staging.at[st, part], landing.at[sl, part])
-        return remote(src, dst, bsend.at[st, i], brecv.at[lax.rem(s, FLAGS), table[k][2] // 2], to)
-
-    def left(s, k):
-        _, staging, i, _, _ = table[k]
+        for part, to in enumerate(LINKS[i][j]):
+            src, dst = staging[i][j].at[st], landing[i][j].at[sl]
+            if len(LINKS[i][j]) > 1:
+                src, dst = src.at[part], dst.at[part]
+            remote(src, dst, bsend.at[st, i, j], brecv.at[lax.rem(s, FLAGS), i, j], to).start()
+
+    def left(s, i, j):
         st = lax.rem(s, 2)
-        sent(staging.at[st], bsend.at[st, i])
-
-    def free_staging(s, copies):
+        sent(staging[i][j].at[st], bsend.at[st, i, j])
+
+    def free_staging(s, i, j):
         @pl.when(s >= 2)
         def _():
-            for k in copies:
-                left(s - 2, k)
-
-    def arrived(s, batch):
-        words = sum(math.prod(table[k][4].shape[1 if table[k][3] is None else 2 :]) for k in BATCHES[batch])
-        sent(w.at[pl.ds(0, words // 256), pl.ds(0, 256)], brecv.at[lax.rem(s, FLAGS), batch])
-
-    def stage1(s):
-        g, cu, cy, sl, st = place(s)
+            left(s - 2, i, j)
+
+    def arrived(s, i, j):
+        _, _, _, sl, _ = place(s)
+        sent(landing[i][j].at[sl], brecv.at[lax.rem(s, FLAGS), i, j])
+
+    def partners(s, h, part):
+        g = s // CHUNKS
 
         @pl.when(lax.rem(s, CHUNKS) == 0)
         def _():
-            for h in range(2):
-                sent(hid.at[pl.ds(g * slots, 4), :, pl.ds(width, width)], hrecv.at[2 * g + h])
-
-        free_staging(s, (0, 2))
+            some = pl.ds(g * slots, len(PARTS[h][part]))
+            sent(hid.at[some, :, pl.ds(width, width)], hrecv.at[2 * g + h, part])
+
+    def u1(s):
+        g, cu, cy, sl, st = place(s)
+
+        partners(s, 0, 0)
+        partners(s, 1, 0)
+        free_staging(s, 0, 0)
         t = term(g, (4, 5), cu, ncu).reshape(2, re, ncu)
         tu1[st, 0] = bf(t[:, :hr])
         tu1[st, 1] = bf(t[:, hr:])
-        for k in (0, 1):
-            bcopy(k, s).start()
-        t = term(g, (1, 3, 5, 7), cy, ncy)
-        ty1[st] = bf(t).reshape(4, re, ncy)
-        bcopy(2, s).start()
-
-    def stage2(s):
-        g, cu, cy, sl, st = place(s)
-        arrived(s, 0)
-        free_staging(s, (3, 5))
+        send(s, 0, 0)
+
+    def y1(s):
+        g, cu, cy, sl, st = place(s)
+        free_staging(s, 1, 0)
+        ty1[st] = bf(term(g, (1, 3, 5, 7), cy, ncy)).reshape(4, re, ncy)
+        send(s, 1, 0)
+
+    def u2(s):
+        g, cu, cy, sl, st = place(s)
+        arrived(s, 0, 0)
+        partners(s, 0, 1)
+        free_staging(s, 0, 1)
         t = term(g, (2, 3), cu, ncu).reshape(2, re, ncu)
         tu2[st, 0, :, :hr] = bf(t[:, :hr] + f32(lu1[sl, 0]))
         tu2[st, 0, :, hr:] = bf(t[:, hr:])
-        bcopy(3, s).start()
         t = term(g, (6, 7), cu, ncu).reshape(2, re, ncu)
         tu2[st, 1, :, :hr] = bf(t[:, :hr])
         tu2[st, 1, :, hr:] = bf(t[:, hr:] + f32(lu1[sl, 1]))
-        bcopy(4, s).start()
+        send(s, 0, 1)
+
+    def y2(s):
+        g, cu, cy, sl, st = place(s)
+        arrived(s, 1, 0)
+        free_staging(s, 1, 1)
         t = term(g, (4,), cy, ncy) + f32(ly1[sl, 2])
         ty2[st, 0] = bf(t[:hr])
         ty2[st, 1] = bf(t[hr:])
-        for k in (5, 6):
-            bcopy(k, s).start()
-
-    def stage3(s):
-        g, cu, cy, sl, st = place(s)
-        arrived(s, 1)
-        free_staging(s, (7, 8))
-        t = term(g, (1,), cu, ncu)
-        tu3[st] = bf(t + f32(lu2[sl, 0, 1]) + f32(lu2[sl, 1, 1]))
-        bcopy(7, s).start()
+        send(s, 1, 1)
+
+    def u3(s):
+        g, cu, cy, sl, st = place(s)
+        arrived(s, 0, 1)
+        free_staging(s, 0, 2)
+        tu3[st] = bf(term(g, (1,), cu, ncu) + f32(lu2[sl, 0, 1]) + f32(lu2[sl, 1, 1]))
+        send(s, 0, 2)
+
+    def y3(s):
+        g, cu, cy, sl, st = place(s)
+        arrived(s, 1, 1)
+        free_staging(s, 1, 2)
         t = term(g, (2, 6), cy, ncy)
         a, b = t[:re] + f32(ly1[sl, 1]), t[re:] + f32(ly1[sl, 3])
         ty3[st, 0, :hr] = bf(a[:hr] + f32(ly2[sl, 0]))
         ty3[st, 0, hr:] = bf(a[hr:])
         ty3[st, 1, :hr] = bf(b[:hr])
         ty3[st, 1, hr:] = bf(b[hr:] + f32(ly2[sl, 1]))
-        for k in (8, 9):
-            bcopy(k, s).start()
+        send(s, 1, 2)
+
+    def u4(s):
+        g, cu, cy, sl, st = place(s)
+        arrived(s, 0, 2)
+        partners(s, 0, 2)
+        finish(s, 0, term(g, (0,), cu, ncu) + f32(lu2[sl, 0, 0]) + f32(lu2[sl, 1, 0]) + f32(lu3[sl]))
+
+    def y4(s):
+        g, cu, cy, sl, st = place(s)
+        arrived(s, 1, 2)
+        finish(s, 1, term(g, (0,), cy, ncy) + f32(ly1[sl, 0]) + f32(ly3[sl, 0]) + f32(ly3[sl, 1]))
 
     def fcopy(s, k):
         g, cu, cy, _, st = place(s)
@@ -491,37 +515,30 @@
         r = pl.ds(pl.multiple_of((g // 2) * re, 8), re)
         cols = pl.ds(pl.multiple_of(role * half + start, LANES), size)
         c = lax.rem(s, CHUNKS)
-        return remote(tq.at[c, :, pl.ds(k * ncu, size)], out.at[r, cols], fsend.at[c], frecv.at[g // 2], "P")
-
-    def stage4(s):
-        g, cu, cy, sl, st = place(s)
-        e, c = g // 2, lax.rem(s, CHUNKS)
-        arrived(s, 2)
+        return remote(tq.at[c, :, pl.ds(k * ncu, size)], out.at[r, cols], fsend.at[c, k], frecv.at[g // 2], "P")
+
+    def finish(s, k, total):
+        g, cu, cy, _, st = place(s)
+        c = lax.rem(s, CHUNKS)
+        start, size = ((cu, ncu), (cy, ncy))[k]
+        piece = tq.at[c, :, pl.ds(k * ncu, size)]
+
+        @pl.when(g == 2)
+        def _():
+            sent(piece, fsend.at[c, k])
 
         @pl.when(lax.rem(g, 2) == 0)
         def _():
-            @pl.when(e > 0)
-            def _():
-                sent(tq.at[c], fsend.at[c])
-
-        tu = term(g, (0,), cu, ncu) + f32(lu2[sl, 0, 0]) + f32(lu2[sl, 1, 0]) + f32(lu3[sl])
-        ty = term(g, (0,), cy, ncy) + f32(ly1[sl, 0]) + f32(ly3[sl, 0]) + f32(ly3[sl, 1])
-
-        @pl.when(lax.rem(g, 2) == 0)
-        def _():
-            tq[c, :, pl.ds(0, ncu)] = bf(tu)
-            tq[c, :, pl.ds(ncu, ncy)] = bf(ty)
+            piece[...] = bf(total)
 
         @pl.when((g == 1) | (g == 2))
         def _():
-            for k in range(2):
-                fcopy(s - CHUNKS * (2 - g), k).start()
+            fcopy(s - CHUNKS * (2 - g), k).start()
 
         @pl.when(lax.rem(g, 2) == 1)
         def _():
-            r = pl.ds(pl.multiple_of(e * re, 8), re)
-            out[r, pl.ds(pl.multiple_of(role * half + cu, LANES), ncu)] = bf(tu)
-            out[r, pl.ds(pl.multiple_of(role * half + cy, LANES), ncy)] = bf(ty)
+            r = pl.ds(pl.multiple_of((g // 2) * re, 8), re)
+            out[r, pl.ds(pl.multiple_of(role * half + start, LANES), size)] = bf(total)
 
     def reduce_step(i):
         @pl.when(i == 0)
@@ -538,7 +555,8 @@
             sent(w.at[pl.ds(0, width), pl.ds(0, quarter)], dsend)
             sent(hid.at[:, :, pl.ds(0, width)], hsend)
 
-        for lag, stage in ((0, stage1), (LAG, stage2), (2 * LAG, stage3), (3 * LAG, stage4)):
+        for (a, b), stage in zip(STAGES, (u1, y1, u2, y2, u3, y3, u4, y4), strict=True):
+            lag = LAGS[a][b]
 
             @pl.when((i >= lag) & (i < steps + lag))
             def _():
@@ -570,10 +588,11 @@
     for e in range(EPOCHS):
         sent(out.at[pl.ds(0, re), pl.ds(0, half)], frecv.at[e])
     for s in (steps - 2, steps - 1):
-        for k in (0, 2, 3, 5, 7, 8):
-            left(s, k)
+        for i, j in STAGES[:-2]:
+            left(s, i, j)
     for c in range(CHUNKS):
-        sent(tq.at[c], fsend.at[c])
+        for k in range(2):
+            sent(tq.at[c, :, pl.ds(k * ncu, (ncu, ncy)[k])], fsend.at[c, k])
 
 
 def solution(mesh):
@@ -614,10 +633,10 @@
                 pltpu.SemaphoreType.DMA,
                 pltpu.SemaphoreType.DMA,
                 pltpu.SemaphoreType.DMA,
-                dma(tasks),
-                dma(2, 6),
-                dma(FLAGS, 3),
-                dma(CHUNKS),
+                dma(tasks, 3),
+                dma(2, 2, 3),
+                dma(FLAGS, 2, 3),
+                dma(CHUNKS, 2),
                 dma(EPOCHS),
             ],
             compiler_params=pltpu.CompilerParams(

time: 353 us -> 349 us (0.989)
  Pallas kernels: 351 us -> 347 us
    pallas_call x1, Pallas kernels: 351 us -> 347 us  [step(): pl.pallas_call(functools.partial(kernel, n, order, msgs), out_shape=(pltp...]
where the time goes in v3:
time: 349 us
  Pallas kernels  347 us (99%)
    pallas_call x1, Pallas kernels, step(): pl.pallas_call(functools.partial(kernel, n, order, msgs), out_shape=(pltp...  347 us

profile of v3, /device:TPU:96, one launch (start us, length us, event | category | flops | bytes accessed | tf_op | source)
XLA Modules:
  0.0 348.6 jit_solution(8747476019501299244)
XLA Ops:
  0.0 347.2 %shard_map.46 = (bf16[160,7168]{1,0:T(8,128)(2,1)S(1)}, bf16[2,8,160,7168]{3,2,1,0:T(8,128)(2,1)}) custom-call(bf16[160,7168]{1,0:T(8,128)(2,1)} %x_hbm.1, bf16[7168,1152]{1,0:T(8,128)(2,1)} %gate_hbm.1, bf16[7168,1152]{1,0:T(8,128)(2,1)} %up_hbm.1, bf16[1152,7168]{1,0:T(8,128)(2,1)} %down_hbm.1), custom_call_target="tpu_custom_call" | custom-call | tf_op jit(solution)/shard_map/pallas_call | solution.py:613
  347.2 1.4 copy.6

commit v4 on v3

--- a/solution.py
+++ b/solution.py
@@ -26,8 +26,8 @@
 VLIM = 64600000
 
 
-FIRST_U, BY_PARTNER = (28, 31), 6
-TUNE = {'due_w': (-2320, 691), 'due_f': (-3850, 1390), 'due_p': 1165, 'due_h': (-390, -1270, -4350, 1830, 870, 12450, 10410, 15370), 'backlog': 6, 'prefer': 48, 'phase': (1, 1, 3, 3), 'hb': 3110, 'blp': 10}
+FIRST_U, BY_PARTNER = (30, 29), 6
+TUNE = {'due_w': (-2685, 675), 'due_f': (-5900, 2080), 'due_p': 1315, 'due_h': (270, 590, 1590, 7110, 5130, 13430, 15010, 26350), 'backlog': 11, 'prefer': 24, 'phase': (0, 0, 2, 1.5), 'hb': 1190, 'blp': 10}
 
 
 def columns(depth):
@@ -88,6 +88,13 @@
 
 def send_kinds(msgs):
     return sorted({kind_of(m) for m in msgs.values()}, key=str)
+
+
+def arrivals_of(msgs, deps):
+    handed_on = set().union(*deps.values())
+    key = {m: m if m in handed_on else (OTHER if v[0] == "P" else v[1], m[2], v[3]) for m, v in msgs.items()}
+    order = {k: i for i, k in enumerate(dict.fromkeys(key.values()))}
+    return key, order
 
 
 def plan(depth, rows, width):
@@ -283,7 +290,7 @@
     for to in link:
         signal(barrier, to)
 
-    index = {name: i for i, name in enumerate(msgs)}
+    key, arrival = arrivals_of(msgs, gather_messages(depth, rows)[1])
     kinds = send_kinds(msgs)
 
     def kind(name):
@@ -297,7 +304,7 @@
         there = OTHER if to == "P" else cls
         block = (pl.ds(r, nr), pl.ds(c, nc))
         return remote(
-            source(cls, src).at[block], xl.at[(there, dst, *block)], gsend.at[kinds.index(kind(name))], grecv.at[index[name]], to
+            source(cls, src).at[block], xl.at[(there, dst, *block)], gsend.at[kinds.index(kind(name))], grecv.at[arrival[key[name]]], to
         )
 
     def xload(t, i):
@@ -336,8 +343,15 @@
         elif kind == "recv" and what[0] == "W":
             wcopy(what[1]).wait_recv()
         elif kind == "recv":
-            gcopy(what).wait_recv()
+            if key[what] == what:
+                gcopy(what).wait_recv()
         elif kind == "load":
+            cls, e, h = tasks[what]
+            slot = TASK_SLOTS[h][op[2]]
+            rest = sum(math.prod(b for _, b in m[4:]) for name, m in msgs.items() if key[name] == (cls, e, slot))
+            if rest:
+                filled = xl.at[cls, slot, pl.ds(e * re, re), pl.ds(0, rest // re)]
+                sent(filled, grecv.at[arrival[cls, e, slot]])
             xload(what, op[2]).start()
         elif kind == "wsend":
             wcopy(what).start()
@@ -607,7 +621,8 @@
         ncu, ncy = 8 * unit // CHUNKS, 6 * unit // CHUNKS
         pieces = half // 2 // 256
         tasks = 4 * EPOCHS
-        pieces_of_sums = (2, 2, hr, ncu), (2, 2, re, ncu), (re, ncu), (4, re, ncy), (2, hr, ncy), (2, re, ncy)
+        two = 2
+        pieces_of_sums = (two, two, hr, ncu), (two, two, re, ncu), (re, ncu), (4, re, ncy), (two, hr, ncy), (two, re, ncy)
         vmem = lambda *shape: pltpu.VMEM(shape, x.dtype)
         dma = lambda *shape: pltpu.SemaphoreType.DMA(shape)
         return pl.pallas_call(
@@ -618,13 +633,13 @@
             scratch_shapes=[
                 vmem(3, depth, 2 * LANES),
                 vmem(2 * width, half),
-                vmem(2, 4 * re, depth),
+                vmem(two, 4 * re, depth),
                 vmem(EPOCHS * n, re, 2 * width),
                 *(vmem(NB, *p) for p in pieces_of_sums),
-                *(vmem(2, *p) for p in pieces_of_sums),
+                *(vmem(two, *p) for p in pieces_of_sums),
                 vmem(CHUNKS, re, ncu + ncy),
                 dma(len(send_kinds(msgs))),
-                dma(len(msgs)),
+                dma(len(arrivals_of(*gather_messages(depth, rows))[1])),
                 dma(2),
                 dma(3),
                 pltpu.SemaphoreType.DMA,
@@ -634,9 +649,9 @@
                 pltpu.SemaphoreType.DMA,
                 pltpu.SemaphoreType.DMA,
                 dma(tasks, 3),
-                dma(2, 2, 3),
-                dma(FLAGS, 2, 3),
-                dma(CHUNKS, 2),
+                dma(two, two, 3),
+                dma(FLAGS, two, 3),
+                dma(CHUNKS, two),
                 dma(EPOCHS),
             ],
             compiler_params=pltpu.CompilerParams(

time: 349 us -> 348 us (level)
  no operation moved by 1% of the time
where the time goes in v4:
time: 348 us
  Pallas kernels  347 us (100%)
    pallas_call x1, Pallas kernels, step(): pl.pallas_call(functools.partial(kernel, n, order, msgs), out_shape=(pltp...  347 us

profile of v4, /device:TPU:96, one launch (start us, length us, event | category | flops | bytes accessed | tf_op | source)
XLA Modules:
  0.0 348.0 jit_solution(17230003865535579471)
XLA Ops:
  0.0 346.6 %shard_map.46 = (bf16[160,7168]{1,0:T(8,128)(2,1)S(1)}, bf16[2,8,160,7168]{3,2,1,0:T(8,128)(2,1)}) custom-call(bf16[160,7168]{1,0:T(8,128)(2,1)} %x_hbm.1, bf16[7168,1152]{1,0:T(8,128)(2,1)} %gate_hbm.1, bf16[7168,1152]{1,0:T(8,128)(2,1)} %up_hbm.1, bf16[1152,7168]{1,0:T(8,128)(2,1)} %down_hbm.1), custom_call_target="tpu_custom_call" | custom-call | tf_op jit(solution)/shard_map/pallas_call | solution.py:628
  346.6 1.4 copy.6

commit v5 on v4

--- a/solution.py
+++ b/solution.py
@@ -334,7 +334,7 @@
         cls, e, _ = tasks[t]
         src = hid.at[(2 * e + 1 - cls) * slots + slot, :, pl.ds(0, width)]
         dst = hid.at[(2 * e + cls) * slots + slot, :, pl.ds(width, width)]
-        return remote(src, dst, hsend, hrecv.at[t, part], "P")
+        return remote(src, dst, hsend, hrecv.at[t // 2, part + 3 * (t % 2)], "P")
 
     def do(op):
         kind, what = op[0], op[1]
@@ -452,7 +452,7 @@
         @pl.when(lax.rem(s, CHUNKS) == 0)
         def _():
             some = pl.ds(g * slots, len(PARTS[h][part]))
-            sent(hid.at[some, :, pl.ds(width, width)], hrecv.at[2 * g + h, part])
+            sent(hid.at[some, :, pl.ds(width, width)], hrecv.at[g, part + 3 * h])
 
     def u1(s):
         g, cu, cy, sl, st = place(s)
@@ -648,7 +648,7 @@
                 pltpu.SemaphoreType.DMA,
                 pltpu.SemaphoreType.DMA,
                 pltpu.SemaphoreType.DMA,
-                dma(tasks, 3),
+                dma(tasks // two, 4),
                 dma(two, two, 3),
                 dma(FLAGS, two, 3),
                 dma(CHUNKS, two),

time: 348 us -> 348 us (level)
  no operation moved by 1% of the time
where the time goes in v5:
time: 348 us
  Pallas kernels  347 us (100%)
    pallas_call x1, Pallas kernels, step(): pl.pallas_call(functools.partial(kernel, n, order, msgs), out_shape=(pltp...  347 us

profile of v5, /device:TPU:96, one launch (start us, length us, event | category | flops | bytes accessed | tf_op | source)
XLA Modules:
  0.0 347.9 jit_solution(1235427671601323525)
XLA Ops:
  0.0 346.5 %shard_map.46 = (bf16[160,7168]{1,0:T(8,128)(2,1)S(1)}, bf16[2,8,160,7168]{3,2,1,0:T(8,128)(2,1)}) custom-call(bf16[160,7168]{1,0:T(8,128)(2,1)} %x_hbm.1, bf16[7168,1152]{1,0:T(8,128)(2,1)} %gate_hbm.1, bf16[7168,1152]{1,0:T(8,128)(2,1)} %up_hbm.1, bf16[1152,7168]{1,0:T(8,128)(2,1)} %down_hbm.1), custom_call_target="tpu_custom_call" | custom-call | tf_op jit(solution)/shard_map/pallas_call | solution.py:628
  346.6 1.4 copy.6
